TPU v7x, 32 devices: a whole 2x2x4 slice. The times are simulated.
32 devices in a mesh: freq: 4 (over y, x), space: 8 (over z, core).
Axes of the slice: x: 2, y: 2, z: 4, core: 2. Of those that a mesh axis runs over, the one named last changes fastest.
Arguments:
- spectra: bfloat16 [64, 24576, 256], P('freq', 'space'), may hold values from -48 to 48, as said below
- weight: float32 [24576], P('space'), may hold values from 0.25 to 4
- partner: int32 [64], P('freq'), may hold values from 0 to 15
- counts: int32 [64], P('freq'), may hold values from 1 to 8
Outputs:
- modes: bfloat16 [64, 16, 24576], P('freq', None, 'space')
- energy: float32 [64, 8], P('freq')
- coherence: float32 [64, 2, 8, 8], P('freq')
Inputs may be any that keep to these rules, and one draw needn't show every extreme that they name: spectra are finite Fourier coefficients.
All inputs are finite; a program needn't handle non-finite values.
Results may differ from a plain program's by a relative error of at most 0.0045.
Values may be sent and summed in bfloat16 or wider, within the bound.
A program may use at most 128 MiB of HBM per device.

v0:
```python
import jax
import jax.numpy as jnp
from jax import lax
from jax.sharding import PartitionSpec as P

KMAX = 8
ITERS = 4


def from_partner(block, axis, apart):
    count = lax.axis_size(axis)
    route = []
    for low in range(count):
        high = low | 1 << apart
        if high != low and high < count:
            route += [(low, high), (high, low)]
    return lax.ppermute(block, axis, route)


def embed(gram_re, gram_im):
    top = jnp.concatenate([gram_re, -gram_im], axis=2)
    bottom = jnp.concatenate([gram_im, gram_re], axis=2)
    return jnp.concatenate([top, bottom], axis=1)


def apply_operator(operator, basis):
    return jnp.einsum("fkc,fdc->fkd", basis, operator, precision=lax.Precision.HIGHEST)


def orthonormal(vectors, half):
    done = []
    for index in range(vectors.shape[1]):
        vector = vectors[:, index, :]
        for earlier in done:
            early_re, early_im = (earlier[:, :half], earlier[:, half:])
            vec_re, vec_im = (vector[:, :half], vector[:, half:])
            proj_re = jnp.sum(early_re * vec_re + early_im * vec_im, axis=1, keepdims=True)
            proj_im = jnp.sum(early_re * vec_im - early_im * vec_re, axis=1, keepdims=True)
            new_re = vec_re - proj_re * early_re + proj_im * early_im
            new_im = vec_im - proj_re * early_im - proj_im * early_re
            vector = jnp.concatenate([new_re, new_im], axis=1)
        length = jnp.sqrt(jnp.sum(vector * vector, axis=1, keepdims=True) + 1e-06)
        done.append(vector / length)
    return jnp.stack(done, axis=1)


def solve(gram_re, gram_im):
    half = gram_re.shape[1]
    operator = embed(gram_re, gram_im)
    basis = jnp.broadcast_to(
        jnp.eye(KMAX, 2 * half, dtype=jnp.float32), (gram_re.shape[0], KMAX, 2 * half)
    )
    for sweep in range(ITERS):
        basis = orthonormal(apply_operator(operator, basis), half)
    image = apply_operator(operator, basis)
    energy = jnp.sum(basis * image, axis=2)
    return (basis, energy)


def combine(moments, half, total):
    gram_re = (moments[:, :half, :half] + moments[:, half:, half:]) / total
    gram_im = (moments[:, :half, half:] - moments[:, half:, :half]) / total
    return (gram_re, gram_im)


def coefficients(basis, energy, counts):
    half = basis.shape[2] // 2
    ranks = jnp.arange(KMAX, dtype=jnp.int32)[None, :]
    scale = jnp.where(ranks < counts[:, None], 1.0 / jnp.sqrt(energy + 1e-06), 0.0)[:, :, None]
    part_re, part_im = (basis[:, :, :half], basis[:, :, half:])
    upper = jnp.concatenate([part_re, -part_im], axis=2) * scale
    lower = jnp.concatenate([part_im, part_re], axis=2) * scale
    return jnp.concatenate([upper, lower], axis=1).astype(jnp.bfloat16)


def cross_terms(own_modes, other_modes, point_weight, total):
    phi = own_modes.astype(jnp.float32)
    psi = other_modes.astype(jnp.float32)
    wphi = phi * point_weight[None, None, :]
    highest = lax.Precision.HIGHEST

    def inner(left, right):
        return jnp.einsum("fkp,flp->fkl", left, right, precision=highest)

    real_part = inner(wphi[:, :KMAX], psi[:, :KMAX]) + inner(wphi[:, KMAX:], psi[:, KMAX:])
    imag_part = inner(wphi[:, :KMAX], psi[:, KMAX:]) - inner(wphi[:, KMAX:], psi[:, :KMAX])
    return jnp.stack([real_part, imag_part], axis=1) / total


def on_device(spectra, weight, partner, counts):
    groups = spectra.shape[0]
    half = spectra.shape[2] // 2
    total = spectra.shape[1] * lax.axis_size("space")
    weighted = (weight[None, :, None] * spectra).astype(jnp.bfloat16)
    moments = lax.dot_general(
        spectra, weighted, (((1,), (1,)), ((0,), (0,))), preferred_element_type=jnp.float32
    )
    summed = lax.psum(moments, "space")
    gram_re, gram_im = combine(summed, half, total)
    basis, energy = solve(gram_re, gram_im)
    coefficient = coefficients(basis, energy, counts)
    modes = jnp.einsum(
        "fkc,fpc->fkp", coefficient, spectra, preferred_element_type=jnp.float32
    ).astype(jnp.bfloat16)
    levels = lax.axis_size("freq").bit_length() - 1
    mirrored = modes
    for bit in range(levels):
        mirrored = from_partner(mirrored, "freq", bit)
    match = (partner[:, None] == jnp.arange(groups, dtype=jnp.int32)[None, :]).astype(jnp.bfloat16)
    chosen = jnp.einsum("fg,gkp->fkp", match, mirrored, preferred_element_type=jnp.float32).astype(
        jnp.bfloat16
    )
    local = cross_terms(modes, chosen, weight, total)
    coherence = lax.psum(local, "space")
    return (modes, energy, coherence)


def solution(mesh):
    in_specs = (P("freq", "space", None), P("space"), P("freq"), P("freq"))
    out_specs = (P("freq", None, "space"), P("freq", None), P("freq", None, None, None))
    return jax.shard_map(
        on_device, mesh=mesh, in_specs=in_specs, out_specs=out_specs, check_vma=False
    )
```

profile of v0, /device:TPU:0, one launch (start us, length us, event | category | flops | bytes accessed | tf_op | source)
XLA Modules:
  0.0 290.2 jit_solution(2149110146235932898)
XLA Ops:
  7.2 20.7 %fusion.2 = f32[16,256,256]{1,2,0:T(8,128)} fusion(bf16[16,3072,256]{2,1,0:T(8,128)(2,1)} %param.4, f32[3072]{0:T(1024)} %param.5), kind=kOutput, calls=%fused_computation.7 | convolution fusion | flops 6480199680 | bytes 29372416 | tf_op jit(solution)/shard_map/dot_general | solution.py:95
  27.9 99.3 %all-reduce.2.cloned.1.call-done = f32[16,256,256]{1,2,0:T(8,128)} async-done(((f32[16,256,256]{1,2,0:T(8,128)}), f32[16,256,256]{1,2,0:T(8,128)}) %all-reduce.2.cloned.1.call-update) | async-done | bytes 4194320 | tf_op jit(solution)/shard_map/psum | solution.py:98
  127.2 2.8 fusion.80
  130.0 1.9 fusion.42
  132.2 0.1 add_reduce_fusion.111
  132.5 0.1 multiply_reduce_fusion.23
  132.7 0.3 add_reduce_fusion.96
  133.0 0.3 add_reduce_fusion.95
  133.4 0.1 multiply_reduce_fusion.22
  133.6 0.3 add_reduce_fusion.89
  133.8 0.2 add_reduce_fusion.94
  134.4 0.3 add_reduce_fusion.88
  134.6 0.2 add_reduce_fusion.102
  135.1 0.3 add_reduce_fusion.87
  135.4 0.3 add_reduce_fusion.86
  136.0 0.2 add_reduce_fusion.85
  136.5 0.2 add_reduce_fusion.84
  137.4 2.0 fusion.40
  140.2 0.3 add_reduce_fusion.68
  140.5 0.3 add_reduce_fusion.67
  141.1 0.3 add_reduce_fusion.61
  141.4 0.2 add_reduce_fusion.66
  141.9 0.3 add_reduce_fusion.60
  142.2 0.2 add_reduce_fusion.74
  142.7 0.3 add_reduce_fusion.59
  142.9 0.3 add_reduce_fusion.58
  143.5 0.2 add_reduce_fusion.57
  144.0 0.2 add_reduce_fusion.56
  145.0 2.0 fusion.38
  147.8 0.3 add_reduce_fusion.40
  148.1 0.3 add_reduce_fusion.39
  148.6 0.3 add_reduce_fusion.33
  148.9 0.2 add_reduce_fusion.38
  149.4 0.3 add_reduce_fusion.32
  149.7 0.2 add_reduce_fusion.46
  150.2 0.3 add_reduce_fusion.31
  150.5 0.3 add_reduce_fusion.30
  151.0 0.2 add_reduce_fusion.29
  151.6 0.2 add_reduce_fusion.28
  152.5 2.2 fusion.36
  155.5 0.3 add_reduce_fusion.12
  155.8 0.3 add_reduce_fusion.11
  156.4 0.3 add_reduce_fusion.5
  156.7 0.2 add_reduce_fusion.10
  157.2 0.3 add_reduce_fusion.4
  157.5 0.2 add_reduce_fusion.18
  157.9 0.3 add_reduce_fusion.3
  158.2 0.3 add_reduce_fusion.2
  158.8 0.2 add_reduce_fusion.1
  159.3 0.2 add_reduce_fusion
  160.3 2.0 fusion.34
  162.5 12.4 %convert_multiply_fusion = (f32[16,16,3072]{2,1,0:T(8,128)S(1)}, bf16[16,16,3072]{2,1,0:T(8,128)(2,1)}) fusion(f32[3072]{0:T(1024)S(1)} %copy-done, bf16[16,3072,256]{2,1,0:T(8,128)(2,1)} %param.4, bf16[16,16,256]{2,0,1:T(8,128)(2,1)S(1)} %pad_maximum_fusion), kind=kOutput, calls=%fused_computation.6 | convolution fusion | flops 405012480 | bytes 30027776 | tf_op jit(solution)/shard_map/fkc,fpc->fkp/dot_general | solution.py:102
  175.0 1.5 collective-permute-start
  176.5 34.6 %collective-permute-done = bf16[16,16,3072]{2,1,0:T(8,128)(2,1)S(1)} collective-permute-done((bf16[16,16,3072]{2,1,0:T(8,128)(2,1)}, bf16[16,16,3072]{2,1,0:T(8,128)(2,1)S(1)}, u32[]{:S(2)}, u32[]{:S(2)}) %collective-permute-start) | collective-permute-done | bytes 1572896 | tf_op jit(solution)/shard_map/ppermute | solution.py:17
  211.1 1.5 collective-permute-start.1
  212.6 33.6 %collective-permute-done.1 = bf16[16,16,3072]{2,1,0:T(8,128)(2,1)S(1)} collective-permute-done((bf16[16,16,3072]{2,1,0:T(8,128)(2,1)S(1)}, bf16[16,16,3072]{2,1,0:T(8,128)(2,1)S(1)}, u32[]{:S(2)}, u32[]{:S(2)}) %collective-permute-start.1) | collective-permute-done | bytes 1572896 | tf_op jit(solution)/shard_map/ppermute | solution.py:17
  246.1 1.9 convolution_convert_fusion
  248.0 0.1 fusion.82
  248.1 1.8 fusion.6
  249.9 1.8 fusion.4
  251.7 1.5 fusion.15
  253.2 1.8 fusion.21
  255.0 27.5 %psum.15 = f32[16,2,8,8]{3,2,0,1:T(8,128)S(1)} all-reduce(f32[16,2,8,8]{3,2,0,1:T(8,128)S(1)} %maximum_multiply_fusion.2), channel_id=1, replica_groups=mesh['freq'=4,'space'=8] {'space'}, use_global_device_ids=true, to_apply=%region_258.259 | all-reduce | flops 2048 | bytes 16384 | tf_op jit(solution)/shard_map/psum | solution.py:114
  282.6 0.7 copy.52
  (199 shorter events, 11.7 us)
Async XLA Ops:
  7.2 120.1 %all-reduce.2.cloned.1.call-start = ((), (), s32[]{:S(2)}) async-start(), calls=%async_computation | async-start | bytes 8388608 | tf_op jit(solution)/shard_map/psum | solution.py:98
  158.5 3.9 %copy-start.2 = (s32[16]{0:T(128)S(1)}, s32[16]{0:T(128)}, u32[]{:S(2)}) copy-start(s32[16]{0:T(128)} %param.7) | copy-start | bytes 196
  160.0 2.6 copy-start
  162.4 12.6 %copy-start.1 = (f32[16,8]{0,1:T(8,128)}, f32[16,8]{0,1:T(8,128)S(1)}, u32[]{:S(2)}) copy-start(f32[16,8]{0,1:T(8,128)S(1)} %fusion.33) | copy-start | bytes 1540
  162.5 83.6 %copy-start.3 = (s32[16]{0:T(128)S(1)}, s32[16]{0:T(128)}, u32[]{:S(2)}) copy-start(s32[16]{0:T(128)} %param.6) | copy-start | bytes 196
  175.0 36.1 %collective-permute-start = (bf16[16,16,3072]{2,1,0:T(8,128)(2,1)}, bf16[16,16,3072]{2,1,0:T(8,128)(2,1)S(1)}, u32[]{:S(2)}, u32[]{:S(2)}) collective-permute-start(bf16[16,16,3072]{2,1,0:T(8,128)(2,1)} %get-tuple-element.649), channel_id=1, source_target_pairs={{0,8},{8,0},{16,24},{24,16},{1,9},{9,1},{17,25},{25,17},{2,10},{10... | collective-permute-start | bytes 4718600 | tf_op jit(solution)/shard_map/ppermute | solution.py:17
  211.1 35.0 %collective-permute-start.1 = (bf16[16,16,3072]{2,1,0:T(8,128)(2,1)S(1)}, bf16[16,16,3072]{2,1,0:T(8,128)(2,1)S(1)}, u32[]{:S(2)}, u32[]{:S(2)}) collective-permute-start(bf16[16,16,3072]{2,1,0:T(8,128)(2,1)S(1)} %collective-permute-done), channel_id=1, source_target_pairs={{0,16},{16,0},{8,24},{24,8},{1,17},{17,1},{9,25},{25,9},{2,18},{18... | collective-permute-start | bytes 4718600 | tf_op jit(solution)/shard_map/ppermute | solution.py:17
Sparse Core Ops, SparseCore 0:
  28.0 99.1 all-reduce.1
where the time goes:
time: 290 us
  waiting for transfers between devices  168 us (58%)
  matrix products  51.8 us (18%)
  blocking collectives  27.5 us (9%)
  other arithmetic  24.4 us (8%)
  between operations  14.6 us (5%)
  starting transfers between devices  2.98 us (1%)
    psum x1, waiting for transfers between devices, on_device(): summed = lax.psum(moments, 'space')  99.3 us
    ppermute x2, waiting for transfers between devices, from_partner(): return lax.ppermute(block, axis, route)  68.2 us
    psum x1, blocking collectives, on_device(): coherence = lax.psum(local, 'space')  27.5 us
    dot_general x1, matrix products, on_device(): lax.dot_general(spectra, weighted, (((1,), (1,)), ((0,), (0,))), preferre...  20.7 us
    dot_general x1, matrix products, on_device(): jnp.einsum('fkc,fpc->fkp', coefficient, spectra, preferred_element_type=j...  12.4 us
    reduce_sum x44, other arithmetic, orthonormal(): jnp.sum(early_re * vec_re + early_im * vec_im, axis=1, keepdims=True)  10.6 us
    dot_general x5, matrix products, apply_operator(): jnp.einsum('fkc,fdc->fkd', basis, operator, precision=lax.Precision.HIGHEST)  9.94 us
    dot_general x4, matrix products, inner(): return jnp.einsum('fkp,flp->fkl', left, right, precision=highest)  6.86 us
  transfers between devices with their start and end apart: 3, of which 3 were waited for; matrix products, arithmetic and copies ran while one was open for 0% of the time, Pallas kernels for 0%

commit v1 on v0

v1 whole, which is shorter than its diff:
```python
import functools

import jax
import jax.numpy as jnp
from jax import lax
from jax.experimental import pallas as pl
from jax.experimental.pallas import tpu as pltpu
from jax.sharding import PartitionSpec as P

KMAX = 8
ITERS = 4
AHEAD = 4
LINK = jnp.bfloat16
MESH = pl.DeviceIdType.MESH
F32 = jnp.float32
BF16 = jnp.bfloat16


def dot(left, right, dims, precision=None):
    return lax.dot_general(
        left, right, (dims, ((), ())), precision=precision, preferred_element_type=F32
    )


def split(value):
    high = value.astype(BF16)
    return high, (value - high.astype(F32)).astype(BF16)


def pack(moments, half):
    real = moments[:half, :half] + moments[half:, half:]
    imag = moments[:half, half:] - moments[half:, :half]
    row = lax.broadcasted_iota(jnp.int32, (half, half), 0)
    col = lax.broadcasted_iota(jnp.int32, (half, half), 1)
    return jnp.where(row <= col, real, imag)


def unpack(packed, half):
    row = lax.broadcasted_iota(jnp.int32, (half, half), 0)
    col = lax.broadcasted_iota(jnp.int32, (half, half), 1)
    other = packed.T
    real = jnp.where(row <= col, packed, other)
    imag = jnp.where(row > col, packed, jnp.where(row < col, -other, 0.0))
    return real, imag


def orthonormal(real, imag):
    row = lax.broadcasted_iota(jnp.int32, real.shape, 0)
    for k in range(KMAX):
        a_re = jnp.broadcast_to(real[k : k + 1, :], real.shape)
        a_im = jnp.broadcast_to(imag[k : k + 1, :], imag.shape)
        norm = jnp.sum(a_re * a_re + a_im * a_im, axis=1, keepdims=True)
        p_re = jnp.sum(a_re * real + a_im * imag, axis=1, keepdims=True)
        p_im = jnp.sum(a_re * imag - a_im * real, axis=1, keepdims=True)
        inverse = 1.0 / jnp.sqrt(norm + 1e-06)
        e_re, e_im = a_re * inverse, a_im * inverse
        q_re, q_im = p_re * inverse, p_im * inverse
        later_re = real - q_re * e_re + q_im * e_im
        later_im = imag - q_re * e_im - q_im * e_re
        real = jnp.where(row > k, later_re, jnp.where(row == k, e_re, real))
        imag = jnp.where(row > k, later_im, jnp.where(row == k, e_im, imag))
    return real, imag


def apply_operator(operator, real, imag, half):
    high, low = split(jnp.concatenate([real, imag], axis=0))
    left = jnp.concatenate([high, high, low], axis=1)
    image = dot(left, operator, ((1,), (0,)))
    new_re = image[:KMAX, :half] + image[KMAX:, half:]
    new_im = image[KMAX:, :half] - image[:KMAX, half:]
    return new_re, new_im


def choose(cross, partner, groups):
    wide = 2 * KMAX * groups
    row = lax.broadcasted_iota(jnp.int32, (wide, wide), 0)
    col = lax.broadcasted_iota(jnp.int32, (wide, wide), 1)
    lane_group = col // (2 * KMAX)
    want = jnp.broadcast_to(partner[:, None, :], (groups, 2 * KMAX, partner.shape[1]))
    want = want.reshape(wide, partner.shape[1])
    kept = jnp.where(lane_group == want, cross, 0.0).reshape(groups, 2, KMAX, wide)
    top = kept[:, 0].reshape(groups * KMAX, wide)
    bottom = kept[:, 1].reshape(groups * KMAX, wide)
    from_place = row % (2 * KMAX)
    to_place = col % (2 * KMAX)
    same = jnp.where(from_place == to_place, 1.0, 0.0)
    swap = jnp.where(
        from_place == to_place + KMAX, 1.0, jnp.where(from_place == to_place - KMAX, -1.0, 0.0)
    )
    highest = lax.Precision.HIGHEST
    folded = dot(top, same, ((1,), (0,)), highest) + dot(bottom, swap, ((1,), (0,)), highest)
    shape = (groups * KMAX, wide)
    row_group = lax.broadcasted_iota(jnp.int32, shape, 0) // KMAX
    column_group = lax.broadcasted_iota(jnp.int32, shape, 1) // (2 * KMAX)
    folded = jnp.where(row_group == column_group, folded, 0.0)
    return jnp.sum(folded.reshape(groups, KMAX, wide), axis=0)


def kernel(
    n_freq, n_space, spectra, weight, partner, counts,
    modes_out, energy_out, coherence_out,
    held, columns, send, recv, message, modes, mirrored, scaled,
    partners, partials, arrived,
    load_sem, store_sem, gram_send, gram_recv, basis_send, basis_recv,
    modes_send, modes_recv, partner_send, partner_recv, part_send, part_recv,
):
    groups, points, width = held.shape
    half = width // 2
    part = points // 2
    own = groups // n_space
    total = points * n_space
    band = lax.axis_index("freq")
    me = lax.axis_index("space")
    opposite = n_freq - 1 - band
    upper = jnp.where(band > opposite, 1, 0)
    mine = pl.multiple_of(upper * part, 128)
    theirs = pl.multiple_of((1 - upper) * part, 128)

    def order(step):
        return lax.rem((me + 1) * own + step, groups)

    def load(step):
        f = order(step)
        return pltpu.make_async_copy(spectra.at[f], held.at[f], load_sem.at[f])

    for step in range(AHEAD):
        load(step).start()

    barrier = pltpu.get_barrier_semaphore()
    for apart in range(1, n_space):
        peer = lax.rem(me + apart, n_space)
        pl.semaphore_signal(barrier, inc=1, device_id=(band, peer), device_id_type=MESH)
    for apart in range(n_space):
        peer = lax.rem(me + apart, n_space)
        pl.semaphore_signal(barrier, inc=1, device_id=(opposite, peer), device_id_type=MESH)

    lane_row = lax.broadcasted_iota(jnp.int32, (groups, 128), 0)
    table = jnp.zeros((groups, 128), jnp.int32)
    for f in range(groups):
        table = jnp.where(lane_row == f, partner[f], table)
    partners[0] = table
    for block in range(points // 128):
        span = pl.ds(block * 128, 128)
        columns[span, :] = jnp.broadcast_to(weight[:, span], (128, 128)).T

    pl.semaphore_wait(barrier, 2 * n_space - 1)

    partner_copy = pltpu.make_async_remote_copy(
        src_ref=partners.at[0], dst_ref=partners.at[1], send_sem=partner_send,
        recv_sem=partner_recv, device_id=(opposite, me), device_id_type=MESH,
    )
    partner_copy.start()

    def gram_copy(f, source):
        owner = f // own
        slot = lax.rem(f, own)
        return pltpu.make_async_remote_copy(
            src_ref=send.at[f], dst_ref=recv.at[source, slot], send_sem=gram_send.at[f],
            recv_sem=gram_recv.at[source, slot], device_id=(band, owner), device_id_type=MESH,
        )

    def gram_step(step, carry):
        f = order(step)

        @pl.when(step + AHEAD < groups)
        def _():
            load(step + AHEAD).start()

        load(step).wait()
        block = held[f]
        scale = columns[...]
        weighted = (jnp.concatenate([scale, scale], axis=1) * block.astype(F32)).astype(BF16)
        packed = pack(dot(block, weighted, ((0,), (0,))), half).astype(LINK)
        owner = f // own

        @pl.when(owner != me)
        def _():
            send[f] = packed
            gram_copy(f, me).start()

        @pl.when(owner == me)
        def _():
            recv[me, lax.rem(f, own)] = packed

        return carry

    lax.fori_loop(0, groups, gram_step, 0)

    for apart in range(1, n_space):
        source = lax.rem(me + apart, n_space)
        for slot in range(own):
            gram_copy(source * own + slot, source).wait_send()
            pltpu.make_async_remote_copy(
                src_ref=send.at[0], dst_ref=recv.at[source, slot], send_sem=gram_send.at[0],
                recv_sem=gram_recv.at[source, slot], device_id=(band, source), device_id_type=MESH,
            ).wait_recv()

    operators, state = [], []
    for slot in range(own):
        packed = recv[0, slot].astype(F32)
        for source in range(1, n_space):
            packed = packed + recv[source, slot].astype(F32)
        real, imag = unpack(packed / total, half)
        high, low = split(jnp.concatenate([real, imag], axis=1))
        operators.append(jnp.concatenate([high, low, high], axis=0))
        state += [real[:KMAX], -imag[:KMAX]]

    def all_orthonormal(state):
        done = []
        for slot in range(own):
            done += orthonormal(state[2 * slot], state[2 * slot + 1])
        return tuple(done)

    def sweep(_, state):
        image = []
        for slot in range(own):
            image += apply_operator(operators[slot], state[2 * slot], state[2 * slot + 1], half)
        return all_orthonormal(image)

    state = lax.fori_loop(0, ITERS - 1, sweep, all_orthonormal(state))

    rank = lax.broadcasted_iota(jnp.int32, (KMAX, half), 0)
    for slot in range(own):
        f = me * own + slot
        real, imag = state[2 * slot], state[2 * slot + 1]
        image_re, image_im = apply_operator(operators[slot], real, imag, half)
        energy = jnp.sum(real * image_re + imag * image_im, axis=1, keepdims=True)
        energy = jnp.broadcast_to(energy, (KMAX, half))
        scale = jnp.where(rank < counts[f], 1.0 / jnp.sqrt(energy + 1e-06), 0.0)
        message[f] = jnp.concatenate([real * scale, imag * scale, energy], axis=0)

    def basis_copy(source, peer):
        span = pl.ds(source * own, own)
        return pltpu.make_async_remote_copy(
            src_ref=message.at[span], dst_ref=message.at[span], send_sem=basis_send.at[peer],
            recv_sem=basis_recv.at[source], device_id=(band, peer), device_id_type=MESH,
        )

    for apart in range(1, n_space):
        basis_copy(me, lax.rem(me + apart, n_space)).start()

    def modes_copy(f):
        return pltpu.make_async_remote_copy(
            src_ref=modes.at[f, :, pl.ds(theirs, part)], dst_ref=mirrored.at[f],
            send_sem=modes_send.at[f], recv_sem=modes_recv.at[f],
            device_id=(opposite, me), device_id_type=MESH,
        )

    def store(f):
        return pltpu.make_async_copy(modes.at[f], modes_out.at[f], store_sem.at[f])

    def modes_step(step, carry):
        f = lax.rem(me * own + step, groups)
        source = f // own

        @pl.when(jnp.logical_and(lax.rem(f, own) == 0, source != me))
        def _():
            basis_copy(source, source).wait_recv()

        basis = message[f]
        real, imag = basis[:KMAX], basis[KMAX : 2 * KMAX]
        coefficient = jnp.concatenate(
            [jnp.concatenate([real, -imag], axis=1), jnp.concatenate([imag, real], axis=1)], axis=0
        ).astype(BF16)
        modes[f] = dot(coefficient, held[f], ((1,), (1,))).astype(BF16)
        modes_copy(f).start()
        store(f).start()
        energy_out[f] = basis[2 * KMAX :]
        weighted = modes[f, :, pl.ds(mine, part)].astype(F32) * weight[:, pl.ds(mine, part)]
        high, low = split(weighted)
        scaled[0, f] = high
        scaled[1, f] = low
        return carry

    lax.fori_loop(0, groups, modes_step, 0)

    def modes_wait(f, carry):
        modes_copy(f).wait_recv()
        return carry

    partner_copy.wait()
    lax.fori_loop(0, groups, modes_wait, 0)
    wide = groups * 2 * KMAX
    psi = mirrored[...].reshape(wide, part)
    cross = dot(scaled[0].reshape(wide, part), psi, ((1,), (1,)))
    cross = (cross + dot(scaled[1].reshape(wide, part), psi, ((1,), (1,)))) / total
    spread = functools.partial(jnp.concatenate, axis=1)
    copies = wide // 128
    partials[0] = choose(cross, spread([partners[0]] * copies), groups)
    partials[1] = choose(cross.T, spread([partners[1]] * copies), groups)

    def part_copy(side, source, peer):
        across = opposite if side else band
        return pltpu.make_async_remote_copy(
            src_ref=partials.at[side], dst_ref=arrived.at[side, source],
            send_sem=part_send.at[side, peer], recv_sem=part_recv.at[side, source],
            device_id=(across, peer), device_id_type=MESH,
        )

    for apart in range(n_space):
        peer = lax.rem(me + apart, n_space)
        part_copy(1, me, peer).start()
        if apart:
            part_copy(0, me, peer).start()

    def drain(f, carry):
        modes_copy(f).wait_send()
        store(f).wait()
        return carry

    lax.fori_loop(0, groups, drain, 0)
    for apart in range(1, n_space):
        basis_copy(me, lax.rem(me + apart, n_space)).wait_send()

    result = partials[0]
    for apart in range(n_space):
        peer = lax.rem(me + apart, n_space)
        part_copy(1, peer, peer).wait()
        result = result + arrived[1, peer]
        if apart:
            part_copy(0, peer, peer).wait()
            result = result + arrived[0, peer]
    coherence_out[...] = result


def on_device(n_freq, n_space, spectra, weight, partner, counts):
    groups, points, width = spectra.shape
    half = width // 2
    own = groups // n_space
    rows = 2 * KMAX
    wide = groups * rows
    dma = pltpu.SemaphoreType.DMA
    vmem = pl.BlockSpec(memory_space=pltpu.VMEM)
    smem = pl.BlockSpec(memory_space=pltpu.SMEM)
    hbm = pl.BlockSpec(memory_space=pltpu.HBM)
    modes, energy, coherence = pl.pallas_call(
        functools.partial(kernel, n_freq, n_space),
        out_shape=(
            jax.ShapeDtypeStruct((groups, rows, points), BF16),
            jax.ShapeDtypeStruct((groups, KMAX, half), F32),
            jax.ShapeDtypeStruct((KMAX, wide), F32),
        ),
        in_specs=[hbm, vmem, smem, smem],
        out_specs=(hbm, vmem, vmem),
        scratch_shapes=[
            pltpu.VMEM((groups, points, width), BF16),
            pltpu.VMEM((points, 128), F32),
            pltpu.VMEM((groups, half, half), LINK),
            pltpu.VMEM((n_space, own, half, half), LINK),
            pltpu.VMEM((groups, 3 * KMAX, half), F32),
            pltpu.VMEM((groups, rows, points), BF16),
            pltpu.VMEM((groups, rows, points // 2), BF16),
            pltpu.VMEM((2, groups, rows, points // 2), BF16),
            pltpu.VMEM((2, groups, 128), jnp.int32),
            pltpu.VMEM((2, KMAX, wide), F32),
            pltpu.VMEM((2, n_space, KMAX, wide), F32),
            dma((groups,)),
            dma((groups,)),
            dma((groups,)),
            dma((n_space, own)),
            dma((n_space,)),
            dma((n_space,)),
            dma((groups,)),
            dma((groups,)),
            dma(()),
            dma(()),
            dma((2, n_space)),
            dma((2, n_space)),
        ],
        compiler_params=pltpu.CompilerParams(
            collective_id=0, has_side_effects=True, vmem_limit_bytes=60 * 1024 * 1024
        ),
    )(spectra, weight.reshape(1, points), partner, counts)
    coherence = coherence.reshape(KMAX, groups, 2, KMAX).transpose(1, 2, 0, 3)
    return modes, energy[:, :, 0], coherence


def solution(mesh):
    in_specs = (P("freq", "space", None), P("space"), P("freq"), P("freq"))
    out_specs = (P("freq", None, "space"), P("freq", None), P("freq", None, None, None))
    return jax.shard_map(
        functools.partial(on_device, mesh.shape["freq"], mesh.shape["space"]),
        mesh=mesh,
        in_specs=in_specs,
        out_specs=out_specs,
        check_vma=False,
    )
```

time: 290 us -> 62.8 us (0.22)
  waiting for transfers between devices: 168 us -> 0 us
  Pallas kernels: 0 us -> 56 us
  matrix products: 51.8 us -> 0 us
  blocking collectives: 27.5 us -> 0 us
  other arithmetic: 24.4 us -> 0 us
  between operations: 14.6 us -> 0.65 us
  local copies, waits for them, and re-layouts: 1.36 us -> 5.9 us
  starting transfers between devices: 2.98 us -> 0 us
    psum x1 -> x0, waiting for transfers between devices: 99.3 us -> none  [on_device(): summed = lax.psum(moments, 'space')]
    ppermute x2 -> x0, waiting for transfers between devices: 68.2 us -> none  [from_partner(): return lax.ppermute(block, axis, route)]
    pallas_call x0 -> x1, Pallas kernels: none -> 56 us  [on_device(): pl.pallas_call(functools.partial(kernel, n_freq, n_space), out_shape=(jax...]
    dot_general x12 -> x0, matrix products: 51.8 us -> none  [the longest x1 20.7 us: on_device(): lax.dot_general(spectra, weighted, (((1,), (1,)), ((0,), (0,))), preferre...]
    psum x1 -> x0, blocking collectives: 27.5 us -> none  [on_device(): coherence = lax.psum(local, 'space')]
    reduce_sum x77 -> x0, other arithmetic: 14.4 us -> none  [the longest x44 10.6 us: orthonormal(): jnp.sum(early_re * vec_re + early_im * vec_im, axis=1, keepdims=True)]
    ppermute x2 -> x0, starting transfers between devices: 2.94 us -> none  [from_partner(): return lax.ppermute(block, axis, route)]
  transfers between devices with their start and end apart: 3 -> 0, of which waited for: 3 -> 0; matrix products, arithmetic and copies ran while one was open for 0% -> 0% of each run, Pallas kernels for 0% -> 0%
where the time goes in v1:
time: 62.8 us; the launch traced here: 62.5 us
  Pallas kernels  56 us (89%)
  local copies, waits for them, and re-layouts  5.9 us (9%)
  between operations  0.65 us (1%)
    pallas_call x1, Pallas kernels, on_device(): pl.pallas_call(functools.partial(kernel, n_freq, n_space), out_shape=(jax...  56 us
    unnamed x2, local copies, waits for them, and re-layouts  3.43 us
    slice x1, local copies, waits for them, and re-layouts, on_device(): return (modes, energy[:, :, 0], coherence)  1.55 us

profile of v1, /device:TPU:0, one launch (start us, length us, event | category | flops | bytes accessed | tf_op | source)
XLA Modules:
  0.0 62.5 jit_solution(7100225365879574821)
XLA Ops:
  0.6 56.0 %shard_map.67 = (bf16[16,16,3072]{2,1,0:T(8,128)(2,1)}, f32[16,8,128]{2,1,0:T(8,128)}, f32[8,256]{1,0:T(8,128)}) custom-call(bf16[16,3072,256]{2,1,0:T(8,128)(2,1)} %spectra.1, f32[1,3072]{1,0:T(1,128)} %bitcast.6, s32[16]{0:T(128)} %partner.1, s32[16]{0:T(128)} %counts.1), custom_call_target="tpu_custom_call" | custom-call | tf_op jit(solution)/shard_map/pallas_call | solution.py:336
  56.6 1.5 %copy.9 = f32[16,8,1]{0,1,2:T(8,128)} copy(f32[16,8,1]{2,1,0:T(8,128)} %bitcast.5) | data formatting | bytes 1024 | tf_op jit(solution)/shard_map/slice | solution.py:375
  58.2 0.9 %reshape.13 = f32[8,16,2,8]{3,2,1,0:T(2,128)S(1)} reshape(f32[8,256]{1,0:T(8,128)} %get-tuple-element.8) | data formatting | bytes 16384 | tf_op jit(solution)/shard_map/reshape | solution.py:374
  59.1 0.7 %copy.10 = f32[16,2,8,8]{0,3,2,1:T(8,128)} copy(f32[16,2,8,8]{3,1,0,2:T(2,128)S(1)} %bitcast.4) | data formatting | bytes 16384
  59.9 2.7 %copy.12 = bf16[16,16,3072]{2,1,0:T(8,128)(2,1)} copy(bf16[16,16,3072]{2,1,0:T(8,128)(2,1)} %get-tuple-element.15) | data formatting | bytes 3145728

commit v2 on v1

--- a/solution.py
+++ b/solution.py
@@ -10,7 +10,6 @@
 KMAX = 8
 ITERS = 4
 AHEAD = 4
-LINK = jnp.bfloat16
 MESH = pl.DeviceIdType.MESH
 F32 = jnp.float32
 BF16 = jnp.bfloat16
@@ -99,9 +98,9 @@
 def kernel(
     n_freq, n_space, spectra, weight, partner, counts,
     modes_out, energy_out, coherence_out,
-    held, columns, send, recv, message, modes, mirrored, scaled,
+    held, columns, send, paired, recv, message, modes, mirrored, scaled,
     partners, partials, arrived,
-    load_sem, store_sem, gram_send, gram_recv, basis_send, basis_recv,
+    load_sem, store_sem, gram_send, gram_recv, mate_recv, basis_send, basis_recv,
     modes_send, modes_recv, partner_send, partner_recv, part_send, part_recv,
 ):
     groups, points, width = held.shape
@@ -116,8 +115,15 @@
     mine = pl.multiple_of(upper * part, 128)
     theirs = pl.multiple_of((1 - upper) * part, 128)
 
+    side = lax.rem(me, 2)
+    chip = me // 2
+    mate = me + 1 - 2 * side
+
     def order(step):
-        return lax.rem((me + 1) * own + step, groups)
+        target = lax.rem(chip + 1 + step // (2 * own), n_space // 2)
+        place = lax.rem(step, 2 * own)
+        parity = jnp.where(place < own, 1 - side, side)
+        return (2 * target + parity) * own + lax.rem(place, own)
 
     def load(step):
         f = order(step)
@@ -159,6 +165,12 @@
             recv_sem=gram_recv.at[source, slot], device_id=(band, owner), device_id_type=MESH,
         )
 
+    def mate_copy(f):
+        return pltpu.make_async_remote_copy(
+            src_ref=send.at[f], dst_ref=paired.at[f], send_sem=gram_send.at[f],
+            recv_sem=mate_recv.at[f], device_id=(band, mate), device_id_type=MESH,
+        )
+
     def gram_step(step, carry):
         f = order(step)
 
@@ -170,36 +182,47 @@
         block = held[f]
         scale = columns[...]
         weighted = (jnp.concatenate([scale, scale], axis=1) * block.astype(F32)).astype(BF16)
-        packed = pack(dot(block, weighted, ((0,), (0,))), half).astype(LINK)
+        packed = pack(dot(block, weighted, ((0,), (0,))), half)
         owner = f // own
-
-        @pl.when(owner != me)
+        same = lax.rem(owner, 2) == side
+
+        @pl.when(jnp.logical_not(same))
         def _():
             send[f] = packed
-            gram_copy(f, me).start()
-
-        @pl.when(owner == me)
+            mate_copy(f).start()
+
+        @pl.when(same)
         def _():
-            recv[me, lax.rem(f, own)] = packed
+            mate_copy(f).wait_recv()
+            both = packed + paired[f]
+
+            @pl.when(owner != me)
+            def _():
+                send[f] = both
+                gram_copy(f, chip).start()
+
+            @pl.when(owner == me)
+            def _():
+                recv[chip, lax.rem(f, own)] = both
 
         return carry
 
     lax.fori_loop(0, groups, gram_step, 0)
 
-    for apart in range(1, n_space):
-        source = lax.rem(me + apart, n_space)
+    for apart in range(1, n_space // 2):
+        source = lax.rem(chip + apart, n_space // 2)
         for slot in range(own):
-            gram_copy(source * own + slot, source).wait_send()
             pltpu.make_async_remote_copy(
                 src_ref=send.at[0], dst_ref=recv.at[source, slot], send_sem=gram_send.at[0],
-                recv_sem=gram_recv.at[source, slot], device_id=(band, source), device_id_type=MESH,
+                recv_sem=gram_recv.at[source, slot],
+                device_id=(band, 2 * source + side), device_id_type=MESH,
             ).wait_recv()
 
     operators, state = [], []
     for slot in range(own):
-        packed = recv[0, slot].astype(F32)
-        for source in range(1, n_space):
-            packed = packed + recv[source, slot].astype(F32)
+        packed = recv[0, slot]
+        for source in range(1, n_space // 2):
+            packed = packed + recv[source, slot]
         real, imag = unpack(packed / total, half)
         high, low = split(jnp.concatenate([real, imag], axis=1))
         operators.append(jnp.concatenate([high, low, high], axis=0))
@@ -249,6 +272,8 @@
     def store(f):
         return pltpu.make_async_copy(modes.at[f], modes_out.at[f], store_sem.at[f])
 
+    diagonal = rank == lax.broadcasted_iota(jnp.int32, (KMAX, half), 1)
+
     def modes_step(step, carry):
         f = lax.rem(me * own + step, groups)
         source = f // own
@@ -265,7 +290,9 @@
         modes[f] = dot(coefficient, held[f], ((1,), (1,))).astype(BF16)
         modes_copy(f).start()
         store(f).start()
-        energy_out[f] = basis[2 * KMAX :]
+        energy_out[pl.ds(f, 1), :] = jnp.sum(
+            jnp.where(diagonal, basis[2 * KMAX :], 0.0), axis=0, keepdims=True
+        )[:, :KMAX]
         weighted = modes[f, :, pl.ds(mine, part)].astype(F32) * weight[:, pl.ds(mine, part)]
         high, low = split(weighted)
         scaled[0, f] = high
@@ -310,7 +337,10 @@
 
     lax.fori_loop(0, groups, drain, 0)
     for apart in range(1, n_space):
-        basis_copy(me, lax.rem(me + apart, n_space)).wait_send()
+        peer = lax.rem(me + apart, n_space)
+        basis_copy(me, peer).wait_send()
+        for slot in range(own):
+            gram_copy(peer * own + slot, chip).wait_send()
 
     result = partials[0]
     for apart in range(n_space):
@@ -320,7 +350,10 @@
         if apart:
             part_copy(0, peer, peer).wait()
             result = result + arrived[0, peer]
-    coherence_out[...] = result
+    for f in range(groups):
+        for kind in range(2):
+            start = (2 * f + kind) * KMAX
+            coherence_out[f, kind] = result[:, start : start + KMAX]
 
 
 def on_device(n_freq, n_space, spectra, weight, partner, counts):
@@ -337,16 +370,17 @@
         functools.partial(kernel, n_freq, n_space),
         out_shape=(
             jax.ShapeDtypeStruct((groups, rows, points), BF16),
-            jax.ShapeDtypeStruct((groups, KMAX, half), F32),
-            jax.ShapeDtypeStruct((KMAX, wide), F32),
+            jax.ShapeDtypeStruct((groups, KMAX), F32),
+            jax.ShapeDtypeStruct((groups, 2, KMAX, KMAX), F32),
         ),
         in_specs=[hbm, vmem, smem, smem],
         out_specs=(hbm, vmem, vmem),
         scratch_shapes=[
             pltpu.VMEM((groups, points, width), BF16),
             pltpu.VMEM((points, 128), F32),
-            pltpu.VMEM((groups, half, half), LINK),
-            pltpu.VMEM((n_space, own, half, half), LINK),
+            pltpu.VMEM((groups, half, half), F32),
+            pltpu.VMEM((groups, half, half), F32),
+            pltpu.VMEM((n_space // 2, own, half, half), F32),
             pltpu.VMEM((groups, 3 * KMAX, half), F32),
             pltpu.VMEM((groups, rows, points), BF16),
             pltpu.VMEM((groups, rows, points // 2), BF16),
@@ -357,7 +391,8 @@
             dma((groups,)),
             dma((groups,)),
             dma((groups,)),
-            dma((n_space, own)),
+            dma((n_space // 2, own)),
+            dma((groups,)),
             dma((n_space,)),
             dma((n_space,)),
             dma((groups,)),
@@ -371,8 +406,7 @@
             collective_id=0, has_side_effects=True, vmem_limit_bytes=60 * 1024 * 1024
         ),
     )(spectra, weight.reshape(1, points), partner, counts)
-    coherence = coherence.reshape(KMAX, groups, 2, KMAX).transpose(1, 2, 0, 3)
-    return modes, energy[:, :, 0], coherence
+    return modes, energy, coherence
 
 
 def solution(mesh):

time: 62.8 us -> 63.4 us (level)
    pallas_call x0 -> x2, local copies, waits for them, and re-layouts: none -> 3 us  [on_device(): pl.pallas_call(functools.partial(kernel, n_freq, n_space), out_shape=(jax...]
    slice x1 -> x0, local copies, waits for them, and re-layouts: 1.55 us -> none  [on_device(): return (modes, energy[:, :, 0], coherence)]
    reshape x1 -> x0, local copies, waits for them, and re-layouts: 0.92 us -> none  [on_device(): coherence = coherence.reshape(KMAX, groups, 2, KMAX).transpose(1, 2, 0, 3)]
    unnamed x2 -> x1, local copies, waits for them, and re-layouts: 3.43 us -> 2.69 us
where the time goes in v2:
time: 63.4 us; the launch traced here: 62.9 us
  Pallas kernels  56.6 us (89%)
  local copies, waits for them, and re-layouts  5.69 us (9%)
  between operations  0.64 us (1%)
    pallas_call x1, Pallas kernels, on_device(): pl.pallas_call(functools.partial(kernel, n_freq, n_space), out_shape=(jax...  56.6 us
    pallas_call x2, local copies, waits for them, and re-layouts, on_device(): pl.pallas_call(functools.partial(kernel, n_freq, n_space), out_shape=(jax...  3 us
    unnamed x1, local copies, waits for them, and re-layouts  2.69 us

profile of v2, /device:TPU:0, one launch (start us, length us, event | category | flops | bytes accessed | tf_op | source)
XLA Modules:
  0.0 62.9 jit_solution(13638714249431909323)
XLA Ops:
  0.6 56.6 %shard_map.67 = (bf16[16,16,3072]{2,1,0:T(8,128)(2,1)}, f32[16,8]{1,0:T(8,128)}, f32[16,2,8,8]{3,2,1,0:T(8,128)}) custom-call(bf16[16,3072,256]{2,1,0:T(8,128)(2,1)} %spectra.1, f32[1,3072]{1,0:T(1,128)} %bitcast.1, s32[16]{0:T(128)} %partner.1, s32[16]{0:T(128)} %counts.1), custom_call_target="tpu_custom_call" | custom-call | tf_op jit(solution)/shard_map/pallas_call | solution.py:369
  57.2 1.4 %copy.7 = f32[16,8]{0,1:T(8,128)} copy(f32[16,8]{1,0:T(8,128)} %get-tuple-element.4) | data formatting | bytes 1024 | tf_op jit(solution)/shard_map/pallas_call | solution.py:369
  58.6 1.6 %copy.8 = f32[16,2,8,8]{0,3,2,1:T(8,128)} copy(f32[16,2,8,8]{3,2,1,0:T(8,128)} %get-tuple-element.5) | data formatting | bytes 16384 | tf_op jit(solution)/shard_map/pallas_call | solution.py:369
  60.2 2.7 %copy.10 = bf16[16,16,3072]{2,1,0:T(8,128)(2,1)} copy(bf16[16,16,3072]{2,1,0:T(8,128)(2,1)} %get-tuple-element.9) | data formatting | bytes 3145728
